TPU v7x, 32 devices: a whole 2x2x4 slice. The times are simulated.
32 devices in a mesh: dp: 8 (over z, x), mp: 4 (over y, core).
Axes of the slice: x: 2, y: 2, z: 4, core: 2. Of those that a mesh axis runs over, the one named last changes fastest.
Arguments:
- grad_blocks: bfloat16 [16, 128, 128], P('dp', None, 'mp'), may hold values from -0.5 to 0.5
- owner_table: int32 [16], replicated, may hold values from 0 to 7, as said below
- prev_stats: float32 [64, 2, 128, 128], P('dp'), as said below
Outputs:
- update: bfloat16 [16, 128, 128], P('dp', None, 'mp')
- new_stats: float32 [64, 2, 128, 128], P('dp')
- inv_roots: float32 [64, 2, 128, 128], P('dp')
Inputs may be any that keep to these rules, and one draw needn't show every extreme that they name: `owner_table`: every entry is a dp index; no index appears more than 8 times, and some index appears exactly 8 times. `prev_stats`: each [128, 128] matrix is symmetric positive semidefinite.
All inputs are finite; a program needn't handle non-finite values.
Results may differ from a plain program's by a relative error of at most 0.001.
Values may be sent and summed in bfloat16 or wider, within the bound.
A program may use at most 64 MiB of HBM per device.

v0:
```python
import jax
import jax.numpy as jnp
from jax import lax
from jax.sharding import PartitionSpec as P

ITERS = 16


STAT_DECAY = 0.75
DAMPING = 0.03


def batch_product(first, second):
    return jnp.einsum("pij,pjk->pik", first, second, precision=lax.Precision.HIGHEST)


def newton_roots(matrices):
    width = matrices.shape[-1]
    identity = jnp.eye(width, dtype=jnp.float32)
    trace_val = jnp.trace(matrices, axis1=1, axis2=2)
    damped = matrices + DAMPING / width * trace_val[:, None, None] * identity
    norm_val = jnp.sqrt(jnp.sum(damped * damped, axis=(1, 2)))
    root_mat = identity * (1.0 / jnp.sqrt(jnp.sqrt(norm_val)))[:, None, None]
    remainder = damped / norm_val[:, None, None]

    def refine(unused, state_pair):
        root_now, rest_now = state_pair
        factor = (5.0 * identity - rest_now) * 0.25
        root_now = batch_product(root_now, factor)
        square = batch_product(factor, factor)
        quartic = batch_product(square, square)
        return (root_now, batch_product(quartic, rest_now))

    root_mat, remainder = lax.fori_loop(0, ITERS, refine, (root_mat, remainder))
    return root_mat


def per_device(grad_blocks, owner_table, prev_stats):
    dev_count = lax.axis_size("dp")
    my_index = lax.axis_index("dp")
    part_count = lax.axis_size("mp")
    part_index = lax.axis_index("mp")
    blk_local = grad_blocks.shape[0]
    width = grad_blocks.shape[1]
    part_width = grad_blocks.shape[2]
    capacity = prev_stats.shape[0]
    block_total = owner_table.shape[0]
    home_owner = lax.dynamic_slice_in_dim(owner_table, my_index * blk_local, blk_local)
    send_mask = jnp.arange(dev_count, dtype=jnp.int32)[:, None] == home_owner[None, :]
    owned_mask = (owner_table == my_index).astype(jnp.int32)
    slot_rank = jnp.cumsum(owned_mask) - owned_mask
    slot_range = jnp.arange(capacity, dtype=jnp.int32)
    picker = ((owned_mask[None, :] == 1) & (slot_rank[None, :] == slot_range[:, None])).astype(
        jnp.bfloat16
    )
    filled = slot_range < jnp.sum(owned_mask)

    def route(blocks):
        return jnp.where(send_mask[:, :, None, None], blocks[None], jnp.zeros((), blocks.dtype))

    def pick(arrived):
        flat = arrived.reshape(block_total, -1)
        chosen = jnp.dot(picker, flat, preferred_element_type=jnp.float32)
        return chosen.astype(jnp.bfloat16).reshape((capacity,) + arrived.shape[2:])

    arrived = lax.all_to_all(route(grad_blocks), "dp", split_axis=0, concat_axis=0, tiled=True)
    whole = lax.all_gather(pick(arrived), "mp", axis=2, tiled=True)
    left_stat = jnp.einsum("rik,rjk->rij", whole, whole, preferred_element_type=jnp.float32)
    right_stat = jnp.einsum("rki,rkj->rij", whole, whole, preferred_element_type=jnp.float32)
    blended = STAT_DECAY * prev_stats + (1.0 - STAT_DECAY) * jnp.stack(
        [left_stat, right_stat], axis=1
    )
    new_stats = jnp.where(filled[:, None, None, None], blended, 0.0)
    identity = jnp.eye(width, dtype=jnp.float32)
    problems = jnp.where(filled[:, None, None, None], blended, identity).reshape(
        2 * capacity, width, width
    )
    share = 2 * capacity // part_count
    my_problems = lax.dynamic_slice_in_dim(problems, part_index * share, share, 0)
    roots_flat = lax.all_gather(newton_roots(my_problems), "mp", axis=0, tiled=True)
    roots = roots_flat.reshape(capacity, 2, width, width)
    inv_roots = jnp.where(filled[:, None, None, None], roots, 0.0)
    whole_wide = whole.astype(jnp.float32)
    precond = jnp.einsum("rij,rjk->rik", roots[:, 0], whole_wide, precision=lax.Precision.HIGHEST)
    precond = jnp.einsum("rij,rjk->rik", precond, roots[:, 1], precision=lax.Precision.HIGHEST)
    spread = jnp.sqrt(jnp.mean(precond * precond, axis=(1, 2)))
    spread = jnp.where(filled, spread, 1.0)
    scaled = (precond / spread[:, None, None]).astype(jnp.bfloat16)
    columns = lax.dynamic_slice_in_dim(scaled, part_index * part_width, part_width, 2)
    outgoing = jnp.dot(picker.T, columns.reshape(capacity, -1), preferred_element_type=jnp.float32)
    outgoing = outgoing.astype(jnp.bfloat16).reshape(dev_count, blk_local, width, part_width)
    returned = lax.all_to_all(outgoing, "dp", split_axis=0, concat_axis=0, tiled=True)
    update = returned[home_owner, jnp.arange(blk_local, dtype=jnp.int32)]
    return (update, new_stats, inv_roots)


def solution(mesh):
    return jax.shard_map(
        per_device,
        mesh=mesh,
        in_specs=(P("dp", None, "mp"), P(), P("dp", None, None, None)),
        out_specs=(P("dp", None, "mp"), P("dp", None, None, None), P("dp", None, None, None)),
        check_vma=False,
    )
```

profile of v0, /device:TPU:0, one launch (start us, length us, event | category | flops | bytes accessed | tf_op | source)
XLA Modules:
  0.0 105.1 jit_solution(8161209467405375428)
XLA Ops:
  7.2 0.7 fusion.27
  7.9 0.7 broadcast_select_fusion.3
  8.7 7.4 %all-to-all-start = ((bf16[8,2,128,32]{2,3,1,0:T(8,128)(2,1)}), bf16[8,2,128,32]{2,3,1,0:T(8,128)(2,1)S(1)}, u32[]{:S(2)}, u32[]{:S(2)}) async-start(bf16[8,2,128,32]{2,3,1,0:T(8,128)(2,1)} %broadcast_select_fusion.3), calls=%async_computation | async-start | bytes 262144 | tf_op jit(solution)/shard_map/all_to_all | solution.py:66
  16.2 0.6 fusion.28
  16.8 0.7 iota_compare_fusion.4
  17.8 5.7 %all-to-all-done = bf16[8,2,128,32]{2,3,1,0:T(8,128)(2,1)S(1)} async-done(((bf16[8,2,128,32]{2,3,1,0:T(8,128)(2,1)}), bf16[8,2,128,32]{2,3,1,0:T(8,128)(2,1)S(1)}, u32[]{:S(2)}, u32[]{:S(2)}) %all-to-all-start) | async-done | bytes 131104 | tf_op jit(solution)/shard_map/all_to_all | solution.py:66
  24.8 5.8 %all_gather.6 = bf16[8,128,128]{1,2,0:T(8,128)(2,1)S(1)} all-gather(bf16[8,128,32]{1,2,0:T(8,128)(2,1)S(1)} %copy.36), channel_id=1, replica_groups=mesh['dp'=8,'mp'=4] {'mp'}, dimensions={2}, use_global_device_ids=true | all-gather | bytes 327680 | tf_op jit(solution)/shard_map/all_gather | solution.py:67
  31.1 0.6 copy-done.1
  32.8 29.5 %while.13 = (s32[]{:T(128)}, f32[4,128,128]{1,2,0:T(8,128)S(1)}, f32[4,128,128]{2,1,0:T(8,128)S(1)}, s32[]{:T(128)}) while((s32[]{:T(128)}, f32[4,128,128]{1,2,0:T(8,128)S(1)}, f32[4,128,128]{2,1,0:T(8,128)S(1)}, s32[]{:T(128)}) %tuple.38), condition=%wide.region_5.6_spmd.clone, body=%wide.region_4.5_spmd.clone.sunk | while | flops 402948096 | bytes 3866677 | solution.py:34
  34.7 0.6 convolution_bitcast_fusion.4
  36.6 0.6 convolution_bitcast_fusion.4
  38.4 0.6 convolution_bitcast_fusion.4
  40.3 0.6 convolution_bitcast_fusion.4
  42.1 0.6 convolution_bitcast_fusion.4
  44.0 0.6 convolution_bitcast_fusion.4
  47.7 0.6 convolution_bitcast_fusion.4
  49.5 0.6 convolution_bitcast_fusion.4
  53.2 0.6 convolution_bitcast_fusion.4
  55.1 0.6 convolution_bitcast_fusion.4
  58.7 0.6 convolution_bitcast_fusion.4
  62.4 0.8 copy.39
  63.2 14.6 %all-gather.2.cloned.1.call-done = f32[16,128,128]{2,1,0:T(8,128)} async-done(((f32[4,128,128]{2,1,0:T(8,128)}), f32[16,128,128]{2,1,0:T(8,128)}) %all-gather.2.cloned.1.call-update) | async-done | bytes 1048592 | tf_op jit(solution)/shard_map/all_gather | solution.py:80
  77.8 1.4 %broadcast_select_fusion = (f32[8,2,128,128]{3,2,0,1:T(8,128)S(1)}, f32[8,2,128,128]{3,2,0,1:T(8,128)S(1)}) fusion(pred[8]{0:T(512)(128)(4,1)S(1)} %iota_compare_fusion.4, f32[16,128,128]{2,1,0:T(8,128)} %all-gather.2.cloned.1.call-done), kind=kLoop, calls=%fused_computation.24 | loop fusion | flops 262144 | bytes 3145736 | tf_op jit(solution)/shard_map/jit(_where)/select_n | solution.py:82
  79.2 0.7 fusion.12
  80.4 1.1 %multiply_reduce_fusion = (f32[8]{0:T(128)S(1)}, f32[8,128,128]{1,2,0:T(8,128)S(1)}) fusion(f32[8,128,128]{2,1,0:T(8,128)S(1)} %fusion.12, f32[8,2,128,128]{3,2,1,0:T(8,128)S(1)} %bitcast.58), kind=kOutput, calls=%fused_computation.26 | convolution fusion | flops 201588736 | bytes 1572896 | tf_op jit(solution)/shard_map/rij,rjk->rik/dot_general | solution.py:85
  81.5 0.7 sqrt_select_fusion
  83.4 0.8 copy.43
  84.2 5.5 %all-to-all-start.1 = ((bf16[8,2,128,32]{2,3,1,0:T(8,128)(2,1)}), bf16[8,2,128,32]{2,3,1,0:T(8,128)(2,1)S(1)}, u32[]{:S(2)}, u32[]{:S(2)}) async-start(bf16[8,2,128,32]{2,3,1,0:T(8,128)(2,1)} %copy.43), calls=%async_computation.1 | async-start | bytes 262144 | tf_op jit(solution)/shard_map/all_to_all | solution.py:92
  89.7 1.0 copy.45
  90.7 1.0 copy.46
  91.8 5.3 %all-to-all-done.1 = bf16[8,2,128,32]{2,3,1,0:T(8,128)(2,1)S(1)} async-done(((bf16[8,2,128,32]{2,3,1,0:T(8,128)(2,1)}), bf16[8,2,128,32]{2,3,1,0:T(8,128)(2,1)S(1)}, u32[]{:S(2)}, u32[]{:S(2)}) %all-to-all-start.1) | async-done | bytes 131104 | tf_op jit(solution)/shard_map/all_to_all | solution.py:92
  97.1 1.2 %gather_fusion = bf16[2,128,32]{1,2,0:T(8,128)(2,1)} fusion(bf16[8,2,128,32]{2,3,1,0:T(8,128)(2,1)S(1)} %all-to-all-done.1, s32[2]{0:T(128)S(1)} %get-tuple-element.58), kind=kCustom, calls=%fused_computation | custom fusion | bytes 32784 | tf_op jit(solution)/shard_map/gather | solution.py:93
  (138 shorter events, 26.7 us)
Async XLA Ops:
  7.2 0.8 copy-start.2
  8.7 7.5 %copy-start.3 = (s32[16]{0:T(128)S(1)}, s32[16]{0:T(128)}, u32[]{:S(2)}) copy-start(s32[16]{0:T(128)} %param.6) | copy-start | bytes 196
  8.7 14.8 %all-to-all-start = ((bf16[8,2,128,32]{2,3,1,0:T(8,128)(2,1)}), bf16[8,2,128,32]{2,3,1,0:T(8,128)(2,1)S(1)}, u32[]{:S(2)}, u32[]{:S(2)}) async-start(bf16[8,2,128,32]{2,3,1,0:T(8,128)(2,1)} %broadcast_select_fusion.3), calls=%async_computation | async-start | bytes 262144 | tf_op jit(solution)/shard_map/all_to_all | solution.py:66
  16.1 61.7 %all-gather.2.cloned.1.call-start = ((), (), s32[]{:S(2)}) async-start(), calls=%async_computation.2 | async-start | bytes 1310720 | tf_op jit(solution)/shard_map/all_gather | solution.py:80
  30.6 1.2 %copy-start.1 = (f32[8,2,128,128]{3,2,1,0:T(8,128)S(1)}, f32[8,2,128,128]{3,2,1,0:T(8,128)}, u32[]{:S(2)}) copy-start(f32[8,2,128,128]{3,2,1,0:T(8,128)} %param.7) | copy-start | bytes 3145732
  79.2 1.2 %copy-start = (f32[16,128,128]{2,1,0:T(8,128)S(1)}, f32[16,128,128]{2,1,0:T(8,128)}, u32[]{:S(2)}) copy-start(f32[16,128,128]{2,1,0:T(8,128)} %all-gather.2.cloned.1.call-done) | copy-start | bytes 3145732
  84.2 12.9 %all-to-all-start.1 = ((bf16[8,2,128,32]{2,3,1,0:T(8,128)(2,1)}), bf16[8,2,128,32]{2,3,1,0:T(8,128)(2,1)S(1)}, u32[]{:S(2)}, u32[]{:S(2)}) async-start(bf16[8,2,128,32]{2,3,1,0:T(8,128)(2,1)} %copy.43), calls=%async_computation.1 | async-start | bytes 262144 | tf_op jit(solution)/shard_map/all_to_all | solution.py:92
Sparse Core Ops, SparseCore 0:
  63.3 14.3 all-gather.1
where the time goes:
time: 106 us; the launch traced here: 105 us
  matrix products  30.4 us (29%)
  waiting for transfers between devices  25.6 us (24%)
  between operations  14.2 us (13%)
  starting transfers between devices  13 us (12%)
  local copies, waits for them, and re-layouts  8.98 us (8%)
  other arithmetic  6.05 us (6%)
  blocking collectives  5.78 us (5%)
  loops' own time  1.06 us (1%)
    dot_general x64, matrix products, batch_product(): jnp.einsum('pij,pjk->pik', first, second, precision=lax.Precision.HIGHEST)  27.7 us
    all_gather x1, waiting for transfers between devices, per_device(): lax.all_gather(newton_roots(my_problems), 'mp', axis=0, tiled=True)  14.6 us
    all_to_all x1, starting transfers between devices, per_device(): lax.all_to_all(route(grad_blocks), 'dp', split_axis=0, concat_axis=0, til...  7.45 us
    all_gather x1, blocking collectives, per_device(): whole = lax.all_gather(pick(arrived), 'mp', axis=2, tiled=True)  5.78 us
    all_to_all x1, waiting for transfers between devices, per_device(): lax.all_to_all(route(grad_blocks), 'dp', split_axis=0, concat_axis=0, til...  5.7 us
    all_to_all x1, starting transfers between devices, per_device(): lax.all_to_all(outgoing, 'dp', split_axis=0, concat_axis=0, tiled=True)  5.51 us
    all_to_all x1, waiting for transfers between devices, per_device(): lax.all_to_all(outgoing, 'dp', split_axis=0, concat_axis=0, tiled=True)  5.29 us
    unnamed x11, local copies, waits for them, and re-layouts  3.42 us
  transfers between devices with their start and end apart: 3, of which 3 were waited for; matrix products, arithmetic and copies ran while one was open for 3% of the time, Pallas kernels for 0%

commit v1 on v0

v1 whole, which is shorter than its diff:
```python
import functools

import jax
import jax.numpy as jnp
from jax import lax
from jax.experimental import pallas as pl
from jax.experimental.pallas import tpu as pltpu
from jax.sharding import PartitionSpec as P

ITERS = 16
STAT_DECAY = 0.75
DAMPING = 0.03
MESH = pl.DeviceIdType.MESH
BF = jnp.bfloat16
F32 = jnp.float32


def eye_of(n, dtype=F32):
    rows = lax.broadcasted_iota(jnp.int32, (n, n), 0)
    cols = lax.broadcasted_iota(jnp.int32, (n, n), 1)
    return (rows == cols).astype(F32).astype(dtype)


def pair(a):
    high = a.astype(BF)
    low = (a - high.astype(F32)).astype(BF)
    return jnp.concatenate([high, low], axis=1)


def twice(a):
    return jnp.concatenate([a, a], axis=0)


def product(left_pair, right_twice):
    out = jnp.dot(left_pair, right_twice, preferred_element_type=F32)
    width = out.shape[1] // 2
    return out[:, :width] + out[:, width:]


def total(a):
    return jnp.sum(jnp.sum(a, axis=1, keepdims=True), axis=0, keepdims=True)


def kernel(
    n_dp, n_mp, owner_ref, grad_ref, prev_hbm,
    upd_ref, nst_hbm, inv_hbm,
    rank_s, quarter, gbuf, hfull, prev, nst, roots, rest, usend, ubuf, obuf, rbuf,
    loc_sem, g_send, g_recv, m_send, m_recv, u_sem, r_sem, o_send, o_recv,
):
    blk_local, width, part = grad_ref.shape
    cap = prev.shape[0]
    half = cap // 2
    nblk = owner_ref.shape[0]
    me = lax.axis_index("dp")
    my = lax.axis_index("mp")
    mate = my + 1 - 2 * lax.rem(my, 2)
    first = half * lax.rem(my, 2)
    my_rows = pl.ds(pl.multiple_of(my * part, part), part)
    mate_rows = pl.ds(pl.multiple_of(mate * part, part), part)

    prev_in = pltpu.make_async_copy(prev_hbm, prev, loc_sem.at[0])
    prev_in.start()

    barrier = pltpu.get_barrier_semaphore()

    def greet(k, c):
        pl.semaphore_signal(
            barrier, inc=1, device_id={"dp": lax.rem(me + k, n_dp)}, device_id_type=MESH
        )
        return c

    lax.fori_loop(1, n_dp, greet, 0)
    for k in range(1, n_mp):
        pl.semaphore_signal(
            barrier, inc=1, device_id={"mp": lax.rem(my + k, n_mp)}, device_id_type=MESH
        )

    eye_bf = eye_of(width, BF)
    for j in range(blk_local):
        quarter[j] = lax.dot_general(
            grad_ref[j], eye_bf, (((0,), (0,)), ((), ())), preferred_element_type=F32
        ).astype(BF)
    gbuf[0] = quarter[...]

    def scan_table(b, carry):
        count = carry[0]
        mine = owner_ref[b] == me
        rank_s[b] = count
        picked = [
            jnp.where(mine & (count == r), b, carry[1 + r]) for r in range(cap)
        ]
        return (count + mine.astype(jnp.int32), *picked)

    found = lax.fori_loop(0, nblk, scan_table, (jnp.int32(0),) * (cap + 1))
    count, picks = found[0], found[1:]

    pl.semaphore_wait(barrier, n_dp - 1 + n_mp - 1)

    def spread_out(k, c):
        pltpu.make_async_remote_copy(
            src_ref=quarter, dst_ref=gbuf.at[k], send_sem=g_send, recv_sem=g_recv,
            device_id={"dp": lax.rem(me + k, n_dp)}, device_id_type=MESH,
        ).start()
        return c

    lax.fori_loop(1, n_dp, spread_out, 0)
    others = gbuf.at[pl.ds(1, n_dp - 1)]
    pltpu.make_async_copy(others, others, g_recv).wait()

    for r in range(cap):
        home = picks[r] // blk_local
        hfull[r, my_rows, :] = gbuf[
            lax.rem(me - home + n_dp, n_dp), picks[r] - home * blk_local
        ]
    mine_q = hfull.at[:, my_rows, :]
    swaps = []
    for k in range(1, n_mp):
        swap = pltpu.make_async_remote_copy(
            src_ref=mine_q, dst_ref=mine_q,
            send_sem=m_send.at[k - 1], recv_sem=m_recv.at[k - 1],
            device_id={"mp": lax.rem(my + k, n_mp)}, device_id_type=MESH,
        )
        swap.start()
        swaps.append(swap)
    prev_in.wait()
    pltpu.make_async_copy(others, others, g_send).wait()
    for k in range(1, n_mp):
        came = hfull.at[:, pl.ds(pl.multiple_of(lax.rem(my - k + n_mp, n_mp) * part, part), part), :]
        pltpu.make_async_copy(came, came, m_recv.at[k - 1]).wait()

    eye = eye_of(width)
    for r in range(cap):
        h = hfull[r]
        left = lax.dot_general(h, h, (((0,), (0,)), ((), ())), preferred_element_type=F32)
        right = lax.dot_general(h, h, (((1,), (1,)), ((), ())), preferred_element_type=F32)
        for side, stat in ((0, left), (1, right)):
            mix = STAT_DECAY * prev[r, side] + (1.0 - STAT_DECAY) * stat
            nst[r, side] = jnp.where(r < count, mix, 0.0)
            prev[r, side] = jnp.where(r < count, mix, eye)
    nst_out = pltpu.make_async_copy(nst, nst_hbm, loc_sem.at[1])
    nst_out.start()

    slots = [(first + i // 2, i % 2) for i in range(2 * half)]
    span = range(2 * half)
    for i in span:
        s = prev[slots[i]]
        a = s + (DAMPING / width) * total(s * eye) * eye
        c = jnp.sqrt(total(a * a))
        roots[slots[i]] = eye * (1.0 / jnp.sqrt(jnp.sqrt(c)))
        rest[i] = a * (1.0 / c)

    def refine(_, carry):
        ident = eye_of(width)
        xs = [roots[slots[i]] for i in span]
        ms = [rest[i] for i in span]
        ml = [pair(m) for m in ms]
        mr = [twice(m) for m in ml]
        out = [product(jnp.concatenate([ml[i], pair(xs[i])], axis=0), mr[i]) for i in span]
        sq = [
            ident * 1.5625 - ms[i] * 0.625 + out[i][:width] * 0.0625 for i in span
        ]
        for i in span:
            roots[slots[i]] = xs[i] * 1.25 - out[i][width:] * 0.25
        sl = [pair(s) for s in sq]
        us = [product(sl[i], mr[i]) for i in span]
        for i in span:
            rest[i] = product(pair(us[i]), twice(sl[i]))
        return carry

    lax.fori_loop(0, ITERS - 1, refine, 0)
    ms = [pair(rest[i]) for i in span]
    out = [product(pair(roots[slots[i]]), twice(ms[i])) for i in span]
    for i in span:
        roots[slots[i]] = roots[slots[i]] * 1.25 - out[i] * 0.25

    r0 = [pair(roots[slots[2 * i]]) for i in range(half)]
    r1 = [pair(roots[slots[2 * i + 1]]) for i in range(half)]
    mid = [
        jnp.dot(r1[i], twice(hfull[first + i]), preferred_element_type=F32)
        for i in range(half)
    ]
    pre = [product(pair(mid[i]), twice(r0[i])) for i in range(half)]
    for i in range(half):
        rms = jnp.sqrt(total(pre[i] * pre[i]) * (1.0 / (width * width)))
        rest[i] = pre[i] / rms
    for i in range(half):
        ubuf[first + i] = rest[i, my_rows, :].astype(BF)
        usend[i] = rest[i, mate_rows, :].astype(BF)
    u_swap = pltpu.make_async_remote_copy(
        src_ref=usend, dst_ref=ubuf.at[pl.ds(first, half)],
        send_sem=u_sem.at[0], recv_sem=u_sem.at[1],
        device_id={"mp": mate}, device_id_type=MESH,
    )
    u_swap.start()
    my_roots = roots.at[pl.ds(first, half)]
    r_swap = pltpu.make_async_remote_copy(
        src_ref=my_roots, dst_ref=my_roots,
        send_sem=r_sem.at[0], recv_sem=r_sem.at[1],
        device_id={"mp": mate}, device_id_type=MESH,
    )
    r_swap.start()
    theirs_u = ubuf.at[pl.ds(half - first, half)]
    pltpu.make_async_copy(theirs_u, theirs_u, u_sem.at[1]).wait()

    def address(k, c):
        home = lax.rem(me + k, n_dp)
        for j in range(blk_local):
            b = home * blk_local + j
            row = jnp.minimum(rank_s[b], cap - 1)
            obuf[k, j] = jnp.where(owner_ref[b] == me, ubuf[row], jnp.zeros((), BF))
        return c

    lax.fori_loop(0, n_dp, address, 0)
    rbuf[0] = obuf[0]

    def give_back(k, c):
        pltpu.make_async_remote_copy(
            src_ref=obuf.at[k], dst_ref=rbuf.at[k], send_sem=o_send, recv_sem=o_recv,
            device_id={"dp": lax.rem(me + k, n_dp)}, device_id_type=MESH,
        ).start()
        return c

    lax.fori_loop(1, n_dp, give_back, 0)

    theirs_r = roots.at[pl.ds(half - first, half)]
    pltpu.make_async_copy(theirs_r, theirs_r, r_sem.at[1]).wait()
    nst_out.wait()
    for r in range(cap):
        for side in range(2):
            nst[r, side] = jnp.where(r < count, roots[r, side], 0.0)
    inv_out = pltpu.make_async_copy(nst, inv_hbm, loc_sem.at[2])
    inv_out.start()

    back = rbuf.at[pl.ds(1, n_dp - 1)]
    pltpu.make_async_copy(back, back, o_recv).wait()
    for j in range(blk_local):
        owner = owner_ref[me * blk_local + j]
        got = rbuf[lax.rem(me - owner + n_dp, n_dp), j]
        upd_ref[j] = lax.dot_general(
            eye_bf, got, (((1,), (1,)), ((), ())), preferred_element_type=F32
        ).astype(BF)

    for swap in swaps:
        swap.wait_send()
    u_swap.wait_send()
    r_swap.wait_send()
    pltpu.make_async_copy(back, back, o_send).wait()
    inv_out.wait()


def solution(mesh):
    n_dp, n_mp = mesh.shape["dp"], mesh.shape["mp"]

    def per_device(grad_blocks, owner_table, prev_stats):
        blk_local, width, part = grad_blocks.shape
        cap = prev_stats.shape[0]
        vmem = pl.BlockSpec(memory_space=pltpu.VMEM)
        hbm = pl.BlockSpec(memory_space=pl.ANY)
        strip = (blk_local, part, width)
        dma = pltpu.SemaphoreType.DMA
        return pl.pallas_call(
            functools.partial(kernel, n_dp, n_mp),
            out_shape=(
                jax.ShapeDtypeStruct(grad_blocks.shape, BF),
                jax.ShapeDtypeStruct(prev_stats.shape, F32),
                jax.ShapeDtypeStruct(prev_stats.shape, F32),
            ),
            in_specs=[pl.BlockSpec(memory_space=pltpu.SMEM), vmem, hbm],
            out_specs=(vmem, hbm, hbm),
            scratch_shapes=[
                pltpu.SMEM((owner_table.shape[0],), jnp.int32),
                pltpu.VMEM(strip, BF),
                pltpu.VMEM((n_dp, *strip), BF),
                pltpu.VMEM((cap, width, width), BF),
                pltpu.VMEM(prev_stats.shape, F32),
                pltpu.VMEM(prev_stats.shape, F32),
                pltpu.VMEM(prev_stats.shape, F32),
                pltpu.VMEM((cap, width, width), F32),
                pltpu.VMEM((cap // 2, part, width), BF),
                pltpu.VMEM((cap, part, width), BF),
                pltpu.VMEM((n_dp, *strip), BF),
                pltpu.VMEM((n_dp, *strip), BF),
                dma((3,)), dma, dma, dma((n_mp - 1,)), dma((n_mp - 1,)),
                dma((2,)), dma((2,)), dma, dma,
            ],
            compiler_params=pltpu.CompilerParams(
                collective_id=0, has_side_effects=True, vmem_limit_bytes=40 << 20
            ),
        )(owner_table, grad_blocks, prev_stats)

    return jax.shard_map(
        per_device,
        mesh=mesh,
        in_specs=(P("dp", None, "mp"), P(), P("dp", None, None, None)),
        out_specs=(P("dp", None, "mp"), P("dp", None, None, None), P("dp", None, None, None)),
        check_vma=False,
    )
```

time: 106 us -> 39.8 us (0.38)
  Pallas kernels: 0 us -> 34.2 us
  matrix products: 30.4 us -> 0 us
  waiting for transfers between devices: 25.6 us -> 0 us
  between operations: 14.2 us -> 0.66 us
  starting transfers between devices: 13 us -> 0 us
  other arithmetic: 6.05 us -> 0 us
  blocking collectives: 5.78 us -> 0 us
  local copies, waits for them, and re-layouts: 8.98 us -> 4.7 us
  loops' own time: 1.06 us -> 0 us
    pallas_call x0 -> x1, Pallas kernels: none -> 34.2 us  [per_device(): pl.pallas_call(functools.partial(kernel, n_dp, n_mp), out_shape=(jax.Shap...]
    dot_general x70 -> x0, matrix products: 30.4 us -> none  [the longest x64 27.7 us: batch_product(): jnp.einsum('pij,pjk->pik', first, second, precision=lax.Precision.HIGHEST)]
    all_gather x1 -> x0, waiting for transfers between devices: 14.6 us -> none  [per_device(): lax.all_gather(newton_roots(my_problems), 'mp', axis=0, tiled=True)]
    all_to_all x2 -> x0, starting transfers between devices: 13 us -> none  [the longest x1 7.45 us: per_device(): lax.all_to_all(route(grad_blocks), 'dp', split_axis=0, concat_axis=0, til...]
    all_to_all x2 -> x0, waiting for transfers between devices: 11 us -> none  [the longest x1 5.7 us: per_device(): lax.all_to_all(route(grad_blocks), 'dp', split_axis=0, concat_axis=0, til...]
    all_gather x1 -> x0, blocking collectives: 5.78 us -> none  [per_device(): whole = lax.all_gather(pick(arrived), 'mp', axis=2, tiled=True)]
    select_n x4 -> x0, other arithmetic: 3.09 us -> none  [the longest x1 1.4 us: per_device(): inv_roots = jnp.where(filled[:, None, None, None], roots, 0.0)]
    reshape x6 -> x0, local copies, waits for them, and re-layouts: 2.34 us -> none  [the longest x2 1.19 us: per_device(): outgoing.astype(jnp.bfloat16)]
  transfers between devices with their start and end apart: 3 -> 0, of which waited for: 3 -> 0; matrix products, arithmetic and copies ran while one was open for 3% -> 0% of each run, Pallas kernels for 0% -> 0%
where the time goes in v1:
time: 39.8 us; the launch traced here: 39.6 us
  Pallas kernels  34.2 us (86%)
  local copies, waits for them, and re-layouts  4.7 us (12%)
  between operations  0.66 us (2%)
    pallas_call x1, Pallas kernels, per_device(): pl.pallas_call(functools.partial(kernel, n_dp, n_mp), out_shape=(jax.Shap...  34.2 us
    unnamed x7, local copies, waits for them, and re-layouts  4 us

profile of v1, /device:TPU:0, one launch (start us, length us, event | category | flops | bytes accessed | tf_op | source)
XLA Modules:
  0.0 39.6 jit_solution(16550033753143650640)
XLA Ops:
  0.6 0.0 copy-start.1
  0.6 0.8 %copy.6.grad_ref = bf16[2,128,32]{2,1,0:T(8,128)(2,1)S(1)} copy(bf16[2,128,32]{1,2,0:T(8,128)(2,1)} %param.3) | data formatting | bytes 32768 | tf_op args[0]
  1.5 0.0 copy-done.1
  1.5 0.0 copy-start
  1.5 1.2 %copy-done = f32[8,2,128,128]{3,2,1,0:T(8,128)S(1)} copy-done((f32[8,2,128,128]{3,2,1,0:T(8,128)S(1)}, f32[8,2,128,128]{3,2,1,0:T(8,128)}, u32[]{:S(2)}) %copy-start) | copy-done | bytes 1048600
  2.7 34.2 %shard_map.58 = (bf16[2,128,32]{2,1,0:T(8,128)(2,1)S(1)}, f32[8,2,128,128]{3,2,1,0:T(8,128)S(1)}, f32[8,2,128,128]{3,2,1,0:T(8,128)S(1)}) custom-call(s32[16]{0:T(128)S(1)} %copy-done.1, bf16[2,128,32]{2,1,0:T(8,128)(2,1)S(1)} %copy.6.grad_ref, f32[8,2,128,128]{3,2,1,0:T(8,128)S(1)} %copy-done), custom_call_target="tpu_custom_call" | custom-call | tf_op jit(solution)/shard_map/pallas_call | solution.py:261
  37.0 0.7 %copy.7 = bf16[2,128,32]{1,2,0:T(8,128)(2,1)} copy(bf16[2,128,32]{2,1,0:T(8,128)(2,1)S(1)} %get-tuple-element.3) | data formatting | bytes 32768 | tf_op jit(solution)/shard_map/pallas_call | solution.py:261
  37.7 1.0 %copy.10 = f32[8,2,128,128]{3,2,1,0:T(8,128)} copy(f32[8,2,128,128]{3,2,1,0:T(8,128)S(1)} %get-tuple-element.10) | data formatting | bytes 2097152
  38.6 1.0 %copy.11 = f32[8,2,128,128]{3,2,1,0:T(8,128)} copy(f32[8,2,128,128]{3,2,1,0:T(8,128)S(1)} %get-tuple-element.11) | data formatting | bytes 2097152
Async XLA Ops:
  0.6 0.9 %copy-start.1 = (s32[16]{0:T(128)S(1)}, s32[16]{0:T(128)}, u32[]{:S(2)}) copy-start(s32[16]{0:T(128)} %owner_ref.1) | copy-start | bytes 196
  1.5 1.2 %copy-start = (f32[8,2,128,128]{3,2,1,0:T(8,128)S(1)}, f32[8,2,128,128]{3,2,1,0:T(8,128)}, u32[]{:S(2)}) copy-start(f32[8,2,128,128]{3,2,1,0:T(8,128)} %prev_hbm.1) | copy-start | bytes 3145732

commit v2 on v1

v2 whole, which is shorter than its diff:
```python
import functools

import jax
import jax.numpy as jnp
from jax import lax
from jax.experimental import pallas as pl
from jax.experimental.pallas import tpu as pltpu
from jax.sharding import PartitionSpec as P

ITERS = 16
STAT_DECAY = 0.75
DAMPING = 0.03
MESH = pl.DeviceIdType.MESH
BF = jnp.bfloat16
F32 = jnp.float32


def eye_of(n, dtype=F32):
    rows = lax.broadcasted_iota(jnp.int32, (n, n), 0)
    cols = lax.broadcasted_iota(jnp.int32, (n, n), 1)
    return (rows == cols).astype(F32).astype(dtype)


def pair(a):
    high = a.astype(BF)
    low = (a - high.astype(F32)).astype(BF)
    return jnp.concatenate([high, low], axis=1)


def twice(a):
    return jnp.concatenate([a, a], axis=0)


def product(left_pair, right_twice):
    out = jnp.dot(left_pair, right_twice, preferred_element_type=F32)
    width = out.shape[1] // 2
    return out[:, :width] + out[:, width:]


def total(a):
    return jnp.sum(jnp.sum(a, axis=1, keepdims=True), axis=0, keepdims=True)


def kernel(
    n_dp, n_mp, owner_ref, grad_ref, prev_hbm,
    upd_ref, nst, inv,
    rank_s, gall, prev, roots, rest, usend, ubuf, obuf, rbuf,
    loc_sem, g_send, g_recv, m_send, m_recv, u_send, u_recv, r_send, r_recv, f_send, f_recv,
    o_send, o_recv,
):
    blk_local, part, width = grad_ref.shape
    cap = prev.shape[0]
    own = cap // n_mp
    nblk = owner_ref.shape[0]
    me = lax.axis_index("dp")
    my = lax.axis_index("mp")
    mate = my + 1 - 2 * lax.rem(my, 2)
    first = own * my
    low_half = me < n_dp // 2

    def rows_of(index):
        return pl.ds(pl.multiple_of(index * part, part), part)

    def slots_of(index):
        return pl.ds(index * own, own)

    def far_first(i):
        return jnp.where(low_half, n_dp - 1 - i, i)

    def offset(d):
        return lax.rem(d - me + n_dp, n_dp)

    def peer(k):
        return lax.rem(my + k, n_mp)

    prev_in = pltpu.make_async_copy(prev_hbm, prev, loc_sem)
    prev_in.start()

    barrier = pltpu.get_barrier_semaphore()

    def greet(k, c):
        pl.semaphore_signal(
            barrier, inc=1, device_id={"dp": lax.rem(me + k, n_dp)}, device_id_type=MESH
        )
        return c

    lax.fori_loop(1, n_dp, greet, 0)
    for k in range(1, n_mp):
        pl.semaphore_signal(barrier, inc=1, device_id={"mp": peer(k)}, device_id_type=MESH)

    my_rows = rows_of(my)
    gall[0, :, my_rows, :] = grad_ref[...]

    def scan_table(b, carry):
        count = carry[0]
        mine = owner_ref[b] == me
        rank_s[b] = count
        picked = [
            jnp.where(mine & (count == r), b, carry[1 + r]) for r in range(cap)
        ]
        return (count + mine.astype(jnp.int32), *picked)

    found = lax.fori_loop(0, nblk, scan_table, (jnp.int32(0),) * (cap + 1))
    count, picks = found[0], found[1:]

    pl.semaphore_wait(barrier, n_dp - 1 + n_mp - 1)

    def spread_out(i, c):
        d = far_first(i)

        @pl.when(d != me)
        def _():
            k = offset(d)
            pltpu.make_async_remote_copy(
                src_ref=grad_ref, dst_ref=gall.at[k, :, my_rows, :],
                send_sem=g_send, recv_sem=g_recv.at[k],
                device_id={"dp": d}, device_id_type=MESH,
            ).start()

        return c

    def pass_on(src, k):
        for j in range(1, n_mp):
            pltpu.make_async_remote_copy(
                src_ref=src, dst_ref=gall.at[k, :, my_rows, :],
                send_sem=m_send.at[j - 1], recv_sem=m_recv.at[j - 1],
                device_id={"mp": peer(j)}, device_id_type=MESH,
            ).start()

    lax.fori_loop(0, n_dp, spread_out, 0)
    pass_on(grad_ref, 0)

    def relay(i, c):
        d = far_first(n_dp - 1 - i)

        @pl.when(d != me)
        def _():
            k = lax.rem(me - d + n_dp, n_dp)
            strip = gall.at[k, :, my_rows, :]
            pltpu.make_async_copy(strip, strip, g_recv.at[k]).wait()
            pass_on(strip, k)

        return c

    lax.fori_loop(0, n_dp, relay, 0)
    prev_in.wait()
    for j in range(1, n_mp):
        came = gall.at[:, :, rows_of(lax.rem(my - j + n_mp, n_mp)), :]
        pltpu.make_async_copy(came, came, m_recv.at[j - 1]).wait()

    def block_of(r):
        home = picks[r] // blk_local
        return gall[lax.rem(me - home + n_dp, n_dp), picks[r] - home * blk_local]

    def pick_at(i):
        b = picks[i]
        for q in range(1, n_mp):
            b = jnp.where(my == q, picks[q * own + i], b)
        home = b // blk_local
        return lax.rem(me - home + n_dp, n_dp), b - home * blk_local

    spots = [pick_at(i) for i in range(own)]
    eye = eye_of(width)
    for r in range(cap):
        h = block_of(r)
        left = lax.dot_general(h, h, (((0,), (0,)), ((), ())), preferred_element_type=F32)
        right = lax.dot_general(h, h, (((1,), (1,)), ((), ())), preferred_element_type=F32)
        for side, stat in ((0, left), (1, right)):
            mix = STAT_DECAY * prev[r, side] + (1.0 - STAT_DECAY) * stat
            nst[r, side] = jnp.where(r < count, mix, 0.0)
            prev[r, side] = jnp.where(r < count, mix, eye)

    slots = [(first + i // 2, i % 2) for i in range(2 * own)]
    span = range(2 * own)
    for i in span:
        s = prev[slots[i]]
        a = s + (DAMPING / width) * total(s * eye) * eye
        c = jnp.sqrt(total(a * a))
        roots[slots[i]] = eye * (1.0 / jnp.sqrt(jnp.sqrt(c)))
        rest[i] = a * (1.0 / c)

    def refine(_, carry):
        ident = eye_of(width)
        xs = [roots[slots[i]] for i in span]
        ms = [rest[i] for i in span]
        ml = [pair(m) for m in ms]
        mr = [twice(m) for m in ml]
        out = [product(jnp.concatenate([ml[i], pair(xs[i])], axis=0), mr[i]) for i in span]
        sq = [
            ident * 1.5625 - ms[i] * 0.625 + out[i][:width] * 0.0625 for i in span
        ]
        for i in span:
            roots[slots[i]] = xs[i] * 1.25 - out[i][width:] * 0.25
        sl = [pair(s) for s in sq]
        us = [product(sl[i], mr[i]) for i in span]
        for i in span:
            rest[i] = product(pair(us[i]), twice(sl[i]))
        return carry

    lax.fori_loop(0, ITERS - 1, refine, 0)
    ms = [pair(rest[i]) for i in span]
    out = [product(pair(roots[slots[i]]), twice(ms[i])) for i in span]
    for i in span:
        roots[slots[i]] = roots[slots[i]] * 1.25 - out[i] * 0.25

    def root_copy(src_owner, to, sems, slot):
        part_of = roots.at[src_owner * own + slot]
        return pltpu.make_async_remote_copy(
            src_ref=part_of, dst_ref=part_of, send_sem=sems[0], recv_sem=sems[1],
            device_id={"mp": to}, device_id_type=MESH,
        )

    r0 = [pair(roots[slots[2 * i]]) for i in range(own)]
    r1 = [pair(roots[slots[2 * i + 1]]) for i in range(own)]
    mids = []
    for i in range(own):
        spot = spots[i]
        mids.append(jnp.dot(r1[i], twice(gall[spot[0], spot[1]]), preferred_element_type=F32))
    pre = [product(pair(mids[i]), twice(r0[i])) for i in range(own)]
    for i in range(own):
        rms = jnp.sqrt(total(pre[i] * pre[i]) * (1.0 / (width * width)))
        rest[i] = pre[i] / rms
    for i in range(own):
        for k in range(n_mp):
            rows = rest[i, rows_of(peer(k)), :].astype(BF)
            if k == 0:
                ubuf[first + i] = rows
            else:
                usend[k - 1, i] = rows
    u_swaps = []
    for k in range(1, n_mp):
        u_swaps.append(pltpu.make_async_remote_copy(
            src_ref=usend.at[k - 1], dst_ref=ubuf.at[slots_of(my)],
            send_sem=u_send.at[k - 1], recv_sem=u_recv.at[k - 1],
            device_id={"mp": peer(k)}, device_id_type=MESH,
        ))
        u_swaps[-1].start()
    root_swaps = []
    for i in range(own):
        for j in range(n_mp // 2):
            to = mate if j == 0 else peer(2 * j)
            root_swaps.append(root_copy(my, to, (r_send.at[j, i], r_recv.at[j, i]), i))
            root_swaps[-1].start()
    for k in range(1, n_mp):
        came = ubuf.at[slots_of(lax.rem(my - k + n_mp, n_mp))]
        pltpu.make_async_copy(came, came, u_recv.at[k - 1]).wait()

    def address(k, c):
        home = lax.rem(me + k, n_dp)
        for j in range(blk_local):
            b = home * blk_local + j
            row = jnp.minimum(rank_s[b], cap - 1)
            obuf[k, j] = jnp.where(owner_ref[b] == me, ubuf[row], jnp.zeros((), BF))
        return c

    lax.fori_loop(0, n_dp, address, 0)
    rbuf[0] = obuf[0]

    def give_back(i, c):
        d = far_first(i)

        @pl.when(d != me)
        def _():
            k = offset(d)
            pltpu.make_async_remote_copy(
                src_ref=obuf.at[k], dst_ref=rbuf.at[k], send_sem=o_send, recv_sem=o_recv,
                device_id={"dp": d}, device_id_type=MESH,
            ).start()

        return c

    lax.fori_loop(0, n_dp, give_back, 0)

    for i in range(own):
        for j in range(1, n_mp // 2):
            source = lax.rem(my - 2 * j + n_mp, n_mp)
            came = roots.at[source * own + i]
            pltpu.make_async_copy(came, came, r_recv.at[j, i]).wait()
            root_swaps.append(root_copy(source, mate, (f_send.at[j - 1, i], f_recv.at[j - 1, i]), i))
            root_swaps[-1].start()
    for i in range(own):
        for j in range(n_mp // 2):
            source = lax.rem(mate - 2 * j + n_mp, n_mp)
            came = roots.at[source * own + i]
            sem = r_recv.at[0, i] if j == 0 else f_recv.at[j - 1, i]
            pltpu.make_async_copy(came, came, sem).wait()
    for r in range(cap):
        for side in range(2):
            inv[r, side] = jnp.where(r < count, roots[r, side], 0.0)

    back = rbuf.at[pl.ds(1, n_dp - 1)]
    pltpu.make_async_copy(back, back, o_recv).wait()
    for j in range(blk_local):
        owner = owner_ref[me * blk_local + j]
        got = rbuf[lax.rem(me - owner + n_dp, n_dp), j]
        upd_ref[j] = got

    for swap in u_swaps + root_swaps:
        swap.wait_send()
    others = gall.at[pl.ds(1, n_dp - 1), :, my_rows, :]
    pltpu.make_async_copy(others, others, g_send).wait()
    for j in range(1, n_mp):
        sent = gall.at[:, :, my_rows, :]
        pltpu.make_async_copy(sent, sent, m_send.at[j - 1]).wait()
    pltpu.make_async_copy(back, back, o_send).wait()


def write_out(upd, nst, inv, upd_out, nst_out, inv_out, sems):
    copies = [
        pltpu.make_async_copy(src, dst, sems.at[i])
        for i, (src, dst) in enumerate(((nst, nst_out), (inv, inv_out), (upd, upd_out)))
    ]
    for copy in copies:
        copy.start()
    for copy in copies:
        copy.wait()


def solution(mesh):
    n_dp, n_mp = mesh.shape["dp"], mesh.shape["mp"]

    def per_device(grad_blocks, owner_table, prev_stats):
        strips = jnp.swapaxes(grad_blocks, 1, 2)
        blk_local, part, width = strips.shape
        cap = prev_stats.shape[0]
        own = cap // n_mp
        vmem = pl.BlockSpec(memory_space=pltpu.VMEM)
        hbm = pl.BlockSpec(memory_space=pltpu.HBM)
        strip = strips.shape
        dma = pltpu.SemaphoreType.DMA
        shapes = (
            jax.ShapeDtypeStruct(strip, BF),
            jax.ShapeDtypeStruct(prev_stats.shape, F32),
            jax.ShapeDtypeStruct(prev_stats.shape, F32),
        )
        held = pl.pallas_call(
            functools.partial(kernel, n_dp, n_mp),
            out_shape=shapes,
            in_specs=[pl.BlockSpec(memory_space=pltpu.SMEM), vmem, hbm],
            out_specs=(vmem, vmem, vmem),
            scratch_shapes=[
                pltpu.SMEM((owner_table.shape[0],), jnp.int32),
                pltpu.VMEM((n_dp, blk_local, width, width), BF),
                pltpu.VMEM(prev_stats.shape, F32),
                pltpu.VMEM(prev_stats.shape, F32),
                pltpu.VMEM((2 * own, width, width), F32),
                pltpu.VMEM((n_mp - 1, own, part, width), BF),
                pltpu.VMEM((cap, part, width), BF),
                pltpu.VMEM((n_dp, *strip), BF),
                pltpu.VMEM((n_dp, *strip), BF),
                dma, dma, dma((n_dp,)), dma((n_mp - 1,)), dma((n_mp - 1,)),
                dma((n_mp - 1,)), dma((n_mp - 1,)),
                dma((n_mp // 2, own)), dma((n_mp // 2, own)),
                dma((n_mp // 2, own)), dma((n_mp // 2, own)), dma, dma,
            ],
            compiler_params=pltpu.CompilerParams(
                collective_id=0, has_side_effects=True, vmem_limit_bytes=32 << 20
            ),
        )(owner_table, strips, prev_stats)
        update, new_stats, inv_roots = pl.pallas_call(
            write_out,
            out_shape=shapes,
            in_specs=[pl.BlockSpec(memory_space=pl.ANY)] * 3,
            out_specs=(hbm, hbm, hbm),
            scratch_shapes=[dma((3,))],
            compiler_params=pltpu.CompilerParams(vmem_limit_bytes=1 << 20),
        )(*held)
        return jnp.swapaxes(update, 1, 2), new_stats, inv_roots

    return jax.shard_map(
        per_device,
        mesh=mesh,
        in_specs=(P("dp", None, "mp"), P(), P("dp", None, None, None)),
        out_specs=(P("dp", None, "mp"), P("dp", None, None, None), P("dp", None, None, None)),
        check_vma=False,
    )
```

time: 39.8 us -> 39.3 us (0.987)
  local copies, waits for them, and re-layouts: 4.7 us -> 2.59 us
  Pallas kernels: 34.2 us -> 35.9 us
    pallas_call x1 -> x2, Pallas kernels: 34.2 us -> 35.9 us  [the longest x1 34.5 us: per_device(): pl.pallas_call(functools.partial(kernel, n_dp, n_mp), out_shape=shapes, i...]
    unnamed x7 -> x6, local copies, waits for them, and re-layouts: 4 us -> 2.59 us
    pallas_call x1 -> x0, local copies, waits for them, and re-layouts: 0.69 us -> none  [per_device(): pl.pallas_call(functools.partial(kernel, n_dp, n_mp), out_shape=(jax.Shap...]
where the time goes in v2:
time: 39.3 us; the launch traced here: 39.1 us
  Pallas kernels  35.9 us (91%)
  local copies, waits for them, and re-layouts  2.59 us (7%)
  between operations  0.65 us (2%)
    pallas_call x1, Pallas kernels, per_device(): pl.pallas_call(functools.partial(kernel, n_dp, n_mp), out_shape=shapes, i...  34.5 us
    unnamed x6, local copies, waits for them, and re-layouts  2.59 us
    pallas_call x1, Pallas kernels, per_device(): pl.pallas_call(write_out, out_shape=shapes, in_specs=[pl.BlockSpec(memory...  1.35 us

profile of v2, /device:TPU:0, one launch (start us, length us, event | category | flops | bytes accessed | tf_op | source)
XLA Modules:
  0.0 39.1 jit_solution(17081837223664772441)
XLA Ops:
  0.6 0.0 copy-start.2
  0.6 0.6 %copy-done.2 = s32[16]{0:T(128)S(1)} copy-done((s32[16]{0:T(128)S(1)}, s32[16]{0:T(128)}, u32[]{:S(2)}) %copy-start.2) | copy-done | bytes 88
  1.3 0.0 copy-start
  1.3 1.2 %copy-done = f32[8,2,128,128]{3,2,1,0:T(8,128)S(1)} copy-done((f32[8,2,128,128]{3,2,1,0:T(8,128)S(1)}, f32[8,2,128,128]{3,2,1,0:T(8,128)}, u32[]{:S(2)}) %copy-start) | copy-done | bytes 1048600
  2.5 0.0 copy-start.1
  2.5 0.7 %copy-done.1 = bf16[2,128,32]{1,2,0:T(8,128)(2,1)S(1)} copy-done((bf16[2,128,32]{1,2,0:T(8,128)(2,1)S(1)}, bf16[2,128,32]{1,2,0:T(8,128)(2,1)}, u32[]{:S(2)}) %copy-start.1) | copy-done | bytes 16408
  3.2 34.5 %shard_map.58 = (bf16[2,32,128]{2,1,0:T(8,128)(2,1)S(1)}, f32[8,2,128,128]{3,2,1,0:T(8,128)S(1)}, f32[8,2,128,128]{3,2,1,0:T(8,128)S(1)}) custom-call(s32[16]{0:T(128)S(1)} %copy-done.2, bf16[2,32,128]{2,1,0:T(8,128)(2,1)S(1)} %bitcast.2, f32[8,2,128,128]{3,2,1,0:T(8,128)S(1)} %copy-done), custom_call_target="tpu_custom_call" | custom-call | tf_op jit(solution)/shard_map/pallas_call | solution.py:336
  37.8 1.3 %shard_map.59 = (bf16[2,32,128]{2,1,0:T(8,128)(2,1)}, f32[8,2,128,128]{3,2,1,0:T(8,128)}, f32[8,2,128,128]{3,2,1,0:T(8,128)}) custom-call(bf16[2,32,128]{2,1,0:T(8,128)(2,1)S(1)} %get-tuple-element.9.upd, f32[8,2,128,128]{3,2,1,0:T(8,128)S(1)} %get-tuple-element.10.nst, f32[8,2,128,128]{3,2,1,0:T(8,128)S(1)} %get-tuple-element.11.inv), custom_call_target="tpu_custom_call" | custom-call | tf_op jit(solution)/shard_map/pallas_call | solution.py:360
Async XLA Ops:
  0.6 0.7 %copy-start.2 = (s32[16]{0:T(128)S(1)}, s32[16]{0:T(128)}, u32[]{:S(2)}) copy-start(s32[16]{0:T(128)} %owner_ref.1) | copy-start | bytes 196
  1.3 1.2 %copy-start = (f32[8,2,128,128]{3,2,1,0:T(8,128)S(1)}, f32[8,2,128,128]{3,2,1,0:T(8,128)}, u32[]{:S(2)}) copy-start(f32[8,2,128,128]{3,2,1,0:T(8,128)} %prev_hbm.1) | copy-start | bytes 3145732
  2.5 0.7 %copy-start.1 = (bf16[2,128,32]{1,2,0:T(8,128)(2,1)S(1)}, bf16[2,128,32]{1,2,0:T(8,128)(2,1)}, u32[]{:S(2)}) copy-start(bf16[2,128,32]{1,2,0:T(8,128)(2,1)} %param.3) | copy-start | bytes 49156

commit v3 on v2

--- a/solution.py
+++ b/solution.py
@@ -44,8 +44,8 @@
 def kernel(
     n_dp, n_mp, owner_ref, grad_ref, prev_hbm,
     upd_ref, nst, inv,
-    rank_s, gall, prev, roots, rest, usend, ubuf, obuf, rbuf,
-    loc_sem, g_send, g_recv, m_send, m_recv, u_send, u_recv, r_send, r_recv, f_send, f_recv,
+    rank_s, gbuf, hfull, hown, prev, roots, rest, usend, ubuf, obuf, rbuf,
+    loc_sem, g_send, g_recv, m_send, m_recv, b_send, b_recv, u_send, u_recv, r_send, r_recv, f_send, f_recv,
     o_send, o_recv,
 ):
     blk_local, part, width = grad_ref.shape
@@ -89,7 +89,7 @@
         pl.semaphore_signal(barrier, inc=1, device_id={"mp": peer(k)}, device_id_type=MESH)
 
     my_rows = rows_of(my)
-    gall[0, :, my_rows, :] = grad_ref[...]
+    gbuf[0] = grad_ref[...]
 
     def scan_table(b, carry):
         count = carry[0]
@@ -112,68 +112,54 @@
         def _():
             k = offset(d)
             pltpu.make_async_remote_copy(
-                src_ref=grad_ref, dst_ref=gall.at[k, :, my_rows, :],
-                send_sem=g_send, recv_sem=g_recv.at[k],
+                src_ref=grad_ref, dst_ref=gbuf.at[k], send_sem=g_send, recv_sem=g_recv,
                 device_id={"dp": d}, device_id_type=MESH,
             ).start()
 
         return c
 
-    def pass_on(src, k):
-        for j in range(1, n_mp):
-            pltpu.make_async_remote_copy(
-                src_ref=src, dst_ref=gall.at[k, :, my_rows, :],
-                send_sem=m_send.at[j - 1], recv_sem=m_recv.at[j - 1],
-                device_id={"mp": peer(j)}, device_id_type=MESH,
-            ).start()
-
     lax.fori_loop(0, n_dp, spread_out, 0)
-    pass_on(grad_ref, 0)
-
-    def relay(i, c):
-        d = far_first(n_dp - 1 - i)
-
-        @pl.when(d != me)
-        def _():
-            k = lax.rem(me - d + n_dp, n_dp)
-            strip = gall.at[k, :, my_rows, :]
-            pltpu.make_async_copy(strip, strip, g_recv.at[k]).wait()
-            pass_on(strip, k)
-
-        return c
-
-    lax.fori_loop(0, n_dp, relay, 0)
+    others = gbuf.at[pl.ds(1, n_dp - 1)]
+    pltpu.make_async_copy(others, others, g_recv).wait()
+
+    for r in range(cap):
+        home = picks[r] // blk_local
+        hfull[r, my_rows, :] = gbuf[
+            lax.rem(me - home + n_dp, n_dp), picks[r] - home * blk_local
+        ]
+    swaps = []
+    for sems, whole in (((m_send, m_recv), False), ((b_send, b_recv), True)):
+        for k in range(1, n_mp):
+            src = hfull.at[:, my_rows, :] if whole else hfull.at[slots_of(peer(k)), my_rows, :]
+            swaps.append(pltpu.make_async_remote_copy(
+                src_ref=src, dst_ref=src if whole else hown.at[:, my_rows, :],
+                send_sem=sems[0].at[k - 1], recv_sem=sems[1].at[k - 1],
+                device_id={"mp": peer(k)}, device_id_type=MESH,
+            ))
+            swaps[-1].start()
+    hown[:, my_rows, :] = hfull[slots_of(my), my_rows, :]
     prev_in.wait()
-    for j in range(1, n_mp):
-        came = gall.at[:, :, rows_of(lax.rem(my - j + n_mp, n_mp)), :]
-        pltpu.make_async_copy(came, came, m_recv.at[j - 1]).wait()
-
-    def block_of(r):
-        home = picks[r] // blk_local
-        return gall[lax.rem(me - home + n_dp, n_dp), picks[r] - home * blk_local]
-
-    def pick_at(i):
-        b = picks[i]
-        for q in range(1, n_mp):
-            b = jnp.where(my == q, picks[q * own + i], b)
-        home = b // blk_local
-        return lax.rem(me - home + n_dp, n_dp), b - home * blk_local
-
-    spots = [pick_at(i) for i in range(own)]
-    eye = eye_of(width)
-    for r in range(cap):
-        h = block_of(r)
+
+    def collect(buffer, sems):
+        for k in range(1, n_mp):
+            came = buffer.at[:, rows_of(lax.rem(my - k + n_mp, n_mp)), :]
+            pltpu.make_async_copy(came, came, sems.at[k - 1]).wait()
+
+    def blend(h, slot):
         left = lax.dot_general(h, h, (((0,), (0,)), ((), ())), preferred_element_type=F32)
         right = lax.dot_general(h, h, (((1,), (1,)), ((), ())), preferred_element_type=F32)
-        for side, stat in ((0, left), (1, right)):
-            mix = STAT_DECAY * prev[r, side] + (1.0 - STAT_DECAY) * stat
-            nst[r, side] = jnp.where(r < count, mix, 0.0)
-            prev[r, side] = jnp.where(r < count, mix, eye)
-
+        return [
+            STAT_DECAY * prev[slot, side] + (1.0 - STAT_DECAY) * stat
+            for side, stat in ((0, left), (1, right))
+        ]
+
+    collect(hown, m_recv)
+    eye = eye_of(width)
     slots = [(first + i // 2, i % 2) for i in range(2 * own)]
     span = range(2 * own)
+    mixes = [m for i in range(own) for m in blend(hown[i], first + i)]
     for i in span:
-        s = prev[slots[i]]
+        s = jnp.where(slots[i][0] < count, mixes[i], eye)
         a = s + (DAMPING / width) * total(s * eye) * eye
         c = jnp.sqrt(total(a * a))
         roots[slots[i]] = eye * (1.0 / jnp.sqrt(jnp.sqrt(c)))
@@ -214,8 +200,7 @@
     r1 = [pair(roots[slots[2 * i + 1]]) for i in range(own)]
     mids = []
     for i in range(own):
-        spot = spots[i]
-        mids.append(jnp.dot(r1[i], twice(gall[spot[0], spot[1]]), preferred_element_type=F32))
+        mids.append(jnp.dot(r1[i], twice(hown[i]), preferred_element_type=F32))
     pre = [product(pair(mids[i]), twice(r0[i])) for i in range(own)]
     for i in range(own):
         rms = jnp.sqrt(total(pre[i] * pre[i]) * (1.0 / (width * width)))
@@ -271,6 +256,11 @@
 
     lax.fori_loop(0, n_dp, give_back, 0)
 
+    collect(hfull, b_recv)
+    for r in range(cap):
+        for side, mix in enumerate(blend(hfull[r], r)):
+            nst[r, side] = jnp.where(r < count, mix, 0.0)
+
     for i in range(own):
         for j in range(1, n_mp // 2):
             source = lax.rem(my - 2 * j + n_mp, n_mp)
@@ -295,13 +285,9 @@
         got = rbuf[lax.rem(me - owner + n_dp, n_dp), j]
         upd_ref[j] = got
 
-    for swap in u_swaps + root_swaps:
+    for swap in swaps + u_swaps + root_swaps:
         swap.wait_send()
-    others = gall.at[pl.ds(1, n_dp - 1), :, my_rows, :]
     pltpu.make_async_copy(others, others, g_send).wait()
-    for j in range(1, n_mp):
-        sent = gall.at[:, :, my_rows, :]
-        pltpu.make_async_copy(sent, sent, m_send.at[j - 1]).wait()
     pltpu.make_async_copy(back, back, o_send).wait()
 
 
@@ -340,7 +326,9 @@
             out_specs=(vmem, vmem, vmem),
             scratch_shapes=[
                 pltpu.SMEM((owner_table.shape[0],), jnp.int32),
-                pltpu.VMEM((n_dp, blk_local, width, width), BF),
+                pltpu.VMEM((n_dp, *strip), BF),
+                pltpu.VMEM((cap, width, width), BF),
+                pltpu.VMEM((own, width, width), BF),
                 pltpu.VMEM(prev_stats.shape, F32),
                 pltpu.VMEM(prev_stats.shape, F32),
                 pltpu.VMEM((2 * own, width, width), F32),
@@ -348,7 +336,8 @@
                 pltpu.VMEM((cap, part, width), BF),
                 pltpu.VMEM((n_dp, *strip), BF),
                 pltpu.VMEM((n_dp, *strip), BF),
-                dma, dma, dma((n_dp,)), dma((n_mp - 1,)), dma((n_mp - 1,)),
+                dma, dma, dma, dma((n_mp - 1,)), dma((n_mp - 1,)),
+                dma((n_mp - 1,)), dma((n_mp - 1,)),
                 dma((n_mp - 1,)), dma((n_mp - 1,)),
                 dma((n_mp // 2, own)), dma((n_mp // 2, own)),
                 dma((n_mp // 2, own)), dma((n_mp // 2, own)), dma, dma,

time: 39.3 us -> 37.1 us (0.944)
  Pallas kernels: 35.9 us -> 33.6 us
    pallas_call x1, Pallas kernels: 34.5 us -> 32.2 us  [per_device(): pl.pallas_call(functools.partial(kernel, n_dp, n_mp), out_shape=shapes, i...]
where the time goes in v3:
time: 37.1 us; the launch traced here: 36.8 us
  Pallas kernels  33.6 us (91%)
  local copies, waits for them, and re-layouts  2.59 us (7%)
  between operations  0.65 us (2%)
    pallas_call x1, Pallas kernels, per_device(): pl.pallas_call(functools.partial(kernel, n_dp, n_mp), out_shape=shapes, i...  32.2 us
    unnamed x6, local copies, waits for them, and re-layouts  2.59 us
    pallas_call x1, Pallas kernels, per_device(): pl.pallas_call(write_out, out_shape=shapes, in_specs=[pl.BlockSpec(memory...  1.35 us

profile of v3, /device:TPU:0, one launch (start us, length us, event | category | flops | bytes accessed | tf_op | source)
XLA Modules:
  0.0 36.8 jit_solution(3127434736890353827)
XLA Ops:
  0.6 0.0 copy-start.2
  0.6 0.6 %copy-done.2 = s32[16]{0:T(128)S(1)} copy-done((s32[16]{0:T(128)S(1)}, s32[16]{0:T(128)}, u32[]{:S(2)}) %copy-start.2) | copy-done | bytes 88
  1.3 0.0 copy-start
  1.3 1.2 %copy-done = f32[8,2,128,128]{3,2,1,0:T(8,128)S(1)} copy-done((f32[8,2,128,128]{3,2,1,0:T(8,128)S(1)}, f32[8,2,128,128]{3,2,1,0:T(8,128)}, u32[]{:S(2)}) %copy-start) | copy-done | bytes 1048600
  2.5 0.0 copy-start.1
  2.5 0.7 %copy-done.1 = bf16[2,128,32]{1,2,0:T(8,128)(2,1)S(1)} copy-done((bf16[2,128,32]{1,2,0:T(8,128)(2,1)S(1)}, bf16[2,128,32]{1,2,0:T(8,128)(2,1)}, u32[]{:S(2)}) %copy-start.1) | copy-done | bytes 16408
  3.2 32.2 %shard_map.58 = (bf16[2,32,128]{2,1,0:T(8,128)(2,1)S(1)}, f32[8,2,128,128]{3,2,1,0:T(8,128)S(1)}, f32[8,2,128,128]{3,2,1,0:T(8,128)S(1)}) custom-call(s32[16]{0:T(128)S(1)} %copy-done.2, bf16[2,32,128]{2,1,0:T(8,128)(2,1)S(1)} %bitcast.2, f32[8,2,128,128]{3,2,1,0:T(8,128)S(1)} %copy-done), custom_call_target="tpu_custom_call" | custom-call | tf_op jit(solution)/shard_map/pallas_call | solution.py:322
  35.5 1.3 %shard_map.59 = (bf16[2,32,128]{2,1,0:T(8,128)(2,1)}, f32[8,2,128,128]{3,2,1,0:T(8,128)}, f32[8,2,128,128]{3,2,1,0:T(8,128)}) custom-call(bf16[2,32,128]{2,1,0:T(8,128)(2,1)S(1)} %get-tuple-element.9.upd, f32[8,2,128,128]{3,2,1,0:T(8,128)S(1)} %get-tuple-element.10.nst, f32[8,2,128,128]{3,2,1,0:T(8,128)S(1)} %get-tuple-element.11.inv), custom_call_target="tpu_custom_call" | custom-call | tf_op jit(solution)/shard_map/pallas_call | solution.py:349
Async XLA Ops:
  0.6 0.7 %copy-start.2 = (s32[16]{0:T(128)S(1)}, s32[16]{0:T(128)}, u32[]{:S(2)}) copy-start(s32[16]{0:T(128)} %owner_ref.1) | copy-start | bytes 196
  1.3 1.2 %copy-start = (f32[8,2,128,128]{3,2,1,0:T(8,128)S(1)}, f32[8,2,128,128]{3,2,1,0:T(8,128)}, u32[]{:S(2)}) copy-start(f32[8,2,128,128]{3,2,1,0:T(8,128)} %prev_hbm.1) | copy-start | bytes 3145732
  2.5 0.7 %copy-start.1 = (bf16[2,128,32]{1,2,0:T(8,128)(2,1)S(1)}, bf16[2,128,32]{1,2,0:T(8,128)(2,1)}, u32[]{:S(2)}) copy-start(bf16[2,128,32]{1,2,0:T(8,128)(2,1)} %param.3) | copy-start | bytes 49156

commit v4 on v3

--- a/solution.py
+++ b/solution.py
@@ -171,19 +171,20 @@
         ms = [rest[i] for i in span]
         ml = [pair(m) for m in ms]
         mr = [twice(m) for m in ml]
-        out = [product(jnp.concatenate([ml[i], pair(xs[i])], axis=0), mr[i]) for i in span]
+        out = [product(ml[i], mr[i]) for i in span]
         sq = [
-            ident * 1.5625 - ms[i] * 0.625 + out[i][:width] * 0.0625 for i in span
+            ident * 1.5625 - ms[i] * 0.625 + out[i] * 0.0625 for i in span
         ]
-        for i in span:
-            roots[slots[i]] = xs[i] * 1.25 - out[i][width:] * 0.25
         sl = [pair(s) for s in sq]
         us = [product(sl[i], mr[i]) for i in span]
+        xm = [product(pair(xs[i]), mr[i]) for i in span]
+        for i in span:
+            roots[slots[i]] = xs[i] * 1.25 - xm[i] * 0.25
         for i in span:
             rest[i] = product(pair(us[i]), twice(sl[i]))
         return carry
 
-    lax.fori_loop(0, ITERS - 1, refine, 0)
+    lax.fori_loop(0, ITERS - 1, refine, 0, unroll=3)
     ms = [pair(rest[i]) for i in span]
     out = [product(pair(roots[slots[i]]), twice(ms[i])) for i in span]
     for i in span:
@@ -343,7 +344,7 @@
                 dma((n_mp // 2, own)), dma((n_mp // 2, own)), dma, dma,
             ],
             compiler_params=pltpu.CompilerParams(
-                collective_id=0, has_side_effects=True, vmem_limit_bytes=32 << 20
+                collective_id=0, has_side_effects=True, vmem_limit_bytes=54_100_000
             ),
         )(owner_table, strips, prev_stats)
         update, new_stats, inv_roots = pl.pallas_call(

time: 37.1 us -> 34.7 us (0.935)
  local copies, waits for them, and re-layouts: 2.59 us -> 1.37 us
  Pallas kernels: 33.6 us -> 32.4 us
    unnamed x6 -> x4, local copies, waits for them, and re-layouts: 2.59 us -> 1.37 us
    pallas_call x1, Pallas kernels: 32.2 us -> 31.1 us  [per_device(): pl.pallas_call(functools.partial(kernel, n_dp, n_mp), out_shape=shapes, i...]
where the time goes in v4:
time: 34.7 us; the launch traced here: 34.5 us
  Pallas kernels  32.4 us (93%)
  local copies, waits for them, and re-layouts  1.37 us (4%)
  between operations  0.65 us (2%)
    pallas_call x1, Pallas kernels, per_device(): pl.pallas_call(functools.partial(kernel, n_dp, n_mp), out_shape=shapes, i...  31.1 us
    unnamed x4, local copies, waits for them, and re-layouts  1.37 us
    pallas_call x1, Pallas kernels, per_device(): pl.pallas_call(write_out, out_shape=shapes, in_specs=[pl.BlockSpec(memory...  1.35 us

profile of v4, /device:TPU:0, one launch (start us, length us, event | category | flops | bytes accessed | tf_op | source)
XLA Modules:
  0.0 34.5 jit_solution(11138108514879679698)
XLA Ops:
  0.6 0.0 copy-start.1
  0.6 0.6 %copy-done.1 = s32[16]{0:T(128)S(1)} copy-done((s32[16]{0:T(128)S(1)}, s32[16]{0:T(128)}, u32[]{:S(2)}) %copy-start.1) | copy-done | bytes 88
  1.3 0.0 copy-start
  1.3 0.7 %copy-done = bf16[2,128,32]{1,2,0:T(8,128)(2,1)S(1)} copy-done((bf16[2,128,32]{1,2,0:T(8,128)(2,1)S(1)}, bf16[2,128,32]{1,2,0:T(8,128)(2,1)}, u32[]{:S(2)}) %copy-start) | copy-done | bytes 16408
  2.0 31.1 %shard_map.58 = (bf16[2,32,128]{2,1,0:T(8,128)(2,1)S(1)}, f32[8,2,128,128]{3,2,1,0:T(8,128)S(1)}, f32[8,2,128,128]{3,2,1,0:T(8,128)S(1)}) custom-call(s32[16]{0:T(128)S(1)} %copy-done.1, bf16[2,32,128]{2,1,0:T(8,128)(2,1)S(1)} %bitcast.2, f32[8,2,128,128]{3,2,1,0:T(8,128)} %prev_hbm.1), custom_call_target="tpu_custom_call" | custom-call | tf_op jit(solution)/shard_map/pallas_call | solution.py:323
  33.1 1.3 %shard_map.59 = (bf16[2,32,128]{2,1,0:T(8,128)(2,1)}, f32[8,2,128,128]{3,2,1,0:T(8,128)}, f32[8,2,128,128]{3,2,1,0:T(8,128)}) custom-call(bf16[2,32,128]{2,1,0:T(8,128)(2,1)S(1)} %get-tuple-element.9.upd, f32[8,2,128,128]{3,2,1,0:T(8,128)S(1)} %get-tuple-element.10.nst, f32[8,2,128,128]{3,2,1,0:T(8,128)S(1)} %get-tuple-element.11.inv), custom_call_target="tpu_custom_call" | custom-call | tf_op jit(solution)/shard_map/pallas_call | solution.py:350
Async XLA Ops:
  0.6 0.7 %copy-start.1 = (s32[16]{0:T(128)S(1)}, s32[16]{0:T(128)}, u32[]{:S(2)}) copy-start(s32[16]{0:T(128)} %owner_ref.1) | copy-start | bytes 196
  1.3 0.7 %copy-start = (bf16[2,128,32]{1,2,0:T(8,128)(2,1)S(1)}, bf16[2,128,32]{1,2,0:T(8,128)(2,1)}, u32[]{:S(2)}) copy-start(bf16[2,128,32]{1,2,0:T(8,128)(2,1)} %param.3) | copy-start | bytes 49156

commit v5 on v4

--- a/solution.py
+++ b/solution.py
@@ -205,7 +205,7 @@
     pre = [product(pair(mids[i]), twice(r0[i])) for i in range(own)]
     for i in range(own):
         rms = jnp.sqrt(total(pre[i] * pre[i]) * (1.0 / (width * width)))
-        rest[i] = pre[i] / rms
+        rest[i] = pre[i] * (1.0 / rms)
     for i in range(own):
         for k in range(n_mp):
             rows = rest[i, rows_of(peer(k)), :].astype(BF)
@@ -262,22 +262,30 @@
         for side, mix in enumerate(blend(hfull[r], r)):
             nst[r, side] = jnp.where(r < count, mix, 0.0)
 
+    def keep(slot):
+        for side in range(2):
+            inv[slot, side] = jnp.where(slot < count, roots[slot, side], 0.0)
+
+    def arrive(source, i, sem):
+        came = roots.at[source * own + i]
+        pltpu.make_async_copy(came, came, sem).wait()
+
+    for i in range(own):
+        keep(first + i)
+        arrive(mate, i, r_recv.at[0, i])
+        keep(mate * own + i)
     for i in range(own):
         for j in range(1, n_mp // 2):
             source = lax.rem(my - 2 * j + n_mp, n_mp)
-            came = roots.at[source * own + i]
-            pltpu.make_async_copy(came, came, r_recv.at[j, i]).wait()
+            arrive(source, i, r_recv.at[j, i])
             root_swaps.append(root_copy(source, mate, (f_send.at[j - 1, i], f_recv.at[j - 1, i]), i))
             root_swaps[-1].start()
-    for i in range(own):
-        for j in range(n_mp // 2):
+            keep(source * own + i)
+    for i in range(own):
+        for j in range(1, n_mp // 2):
             source = lax.rem(mate - 2 * j + n_mp, n_mp)
-            came = roots.at[source * own + i]
-            sem = r_recv.at[0, i] if j == 0 else f_recv.at[j - 1, i]
-            pltpu.make_async_copy(came, came, sem).wait()
-    for r in range(cap):
-        for side in range(2):
-            inv[r, side] = jnp.where(r < count, roots[r, side], 0.0)
+            arrive(source, i, f_recv.at[j - 1, i])
+            keep(source * own + i)
 
     back = rbuf.at[pl.ds(1, n_dp - 1)]
     pltpu.make_async_copy(back, back, o_recv).wait()

time: 34.7 us -> 34.7 us (level)
  no operation moved by 1% of the time
where the time goes in v5:
time: 34.7 us; the launch traced here: 34.5 us
  Pallas kernels  32.5 us (94%)
  local copies, waits for them, and re-layouts  1.37 us (4%)
  between operations  0.65 us (2%)
    pallas_call x1, Pallas kernels, per_device(): pl.pallas_call(functools.partial(kernel, n_dp, n_mp), out_shape=shapes, i...  31.1 us
    unnamed x4, local copies, waits for them, and re-layouts  1.37 us
    pallas_call x1, Pallas kernels, per_device(): pl.pallas_call(write_out, out_shape=shapes, in_specs=[pl.BlockSpec(memory...  1.35 us

profile of v5, /device:TPU:0, one launch (start us, length us, event | category | flops | bytes accessed | tf_op | source)
XLA Modules:
  0.0 34.5 jit_solution(7774530653889866080)
XLA Ops:
  0.6 0.0 copy-start.1
  0.6 0.6 %copy-done.1 = s32[16]{0:T(128)S(1)} copy-done((s32[16]{0:T(128)S(1)}, s32[16]{0:T(128)}, u32[]{:S(2)}) %copy-start.1) | copy-done | bytes 88
  1.3 0.0 copy-start
  1.3 0.7 %copy-done = bf16[2,128,32]{1,2,0:T(8,128)(2,1)S(1)} copy-done((bf16[2,128,32]{1,2,0:T(8,128)(2,1)S(1)}, bf16[2,128,32]{1,2,0:T(8,128)(2,1)}, u32[]{:S(2)}) %copy-start) | copy-done | bytes 16408
  2.0 31.1 %shard_map.58 = (bf16[2,32,128]{2,1,0:T(8,128)(2,1)S(1)}, f32[8,2,128,128]{3,2,1,0:T(8,128)S(1)}, f32[8,2,128,128]{3,2,1,0:T(8,128)S(1)}) custom-call(s32[16]{0:T(128)S(1)} %copy-done.1, bf16[2,32,128]{2,1,0:T(8,128)(2,1)S(1)} %bitcast.2, f32[8,2,128,128]{3,2,1,0:T(8,128)} %prev_hbm.1), custom_call_target="tpu_custom_call" | custom-call | tf_op jit(solution)/shard_map/pallas_call | solution.py:331
  33.1 1.3 %shard_map.59 = (bf16[2,32,128]{2,1,0:T(8,128)(2,1)}, f32[8,2,128,128]{3,2,1,0:T(8,128)}, f32[8,2,128,128]{3,2,1,0:T(8,128)}) custom-call(bf16[2,32,128]{2,1,0:T(8,128)(2,1)S(1)} %get-tuple-element.9.upd, f32[8,2,128,128]{3,2,1,0:T(8,128)S(1)} %get-tuple-element.10.nst, f32[8,2,128,128]{3,2,1,0:T(8,128)S(1)} %get-tuple-element.11.inv), custom_call_target="tpu_custom_call" | custom-call | tf_op jit(solution)/shard_map/pallas_call | solution.py:358
Async XLA Ops:
  0.6 0.7 %copy-start.1 = (s32[16]{0:T(128)S(1)}, s32[16]{0:T(128)}, u32[]{:S(2)}) copy-start(s32[16]{0:T(128)} %owner_ref.1) | copy-start | bytes 196
  1.3 0.7 %copy-start = (bf16[2,128,32]{1,2,0:T(8,128)(2,1)S(1)}, bf16[2,128,32]{1,2,0:T(8,128)(2,1)}, u32[]{:S(2)}) copy-start(bf16[2,128,32]{1,2,0:T(8,128)(2,1)} %param.3) | copy-start | bytes 49156

commit v6 on v4

--- a/solution.py
+++ b/solution.py
@@ -184,7 +184,7 @@
             rest[i] = product(pair(us[i]), twice(sl[i]))
         return carry
 
-    lax.fori_loop(0, ITERS - 1, refine, 0, unroll=3)
+    lax.fori_loop(0, ITERS - 1, refine, 0, unroll=5)
     ms = [pair(rest[i]) for i in span]
     out = [product(pair(roots[slots[i]]), twice(ms[i])) for i in span]
     for i in span:
@@ -223,7 +223,7 @@
         u_swaps[-1].start()
     root_swaps = []
     for i in range(own):
-        for j in range(n_mp // 2):
+        for j in reversed(range(n_mp // 2)):
             to = mate if j == 0 else peer(2 * j)
             root_swaps.append(root_copy(my, to, (r_send.at[j, i], r_recv.at[j, i]), i))
             root_swaps[-1].start()

time: 34.7 us -> 34.6 us (level)
  no operation moved by 1% of the time
where the time goes in v6:
time: 34.6 us; the launch traced here: 34.3 us
  Pallas kernels  32.3 us (93%)
  local copies, waits for them, and re-layouts  1.37 us (4%)
  between operations  0.65 us (2%)
    pallas_call x1, Pallas kernels, per_device(): pl.pallas_call(functools.partial(kernel, n_dp, n_mp), out_shape=shapes, i...  31 us
    unnamed x4, local copies, waits for them, and re-layouts  1.37 us
    pallas_call x1, Pallas kernels, per_device(): pl.pallas_call(write_out, out_shape=shapes, in_specs=[pl.BlockSpec(memory...  1.35 us

profile of v6, /device:TPU:0, one launch (start us, length us, event | category | flops | bytes accessed | tf_op | source)
XLA Modules:
  0.0 34.3 jit_solution(1739918202667909068)
XLA Ops:
  0.6 0.0 copy-start.1
  0.6 0.6 %copy-done.1 = s32[16]{0:T(128)S(1)} copy-done((s32[16]{0:T(128)S(1)}, s32[16]{0:T(128)}, u32[]{:S(2)}) %copy-start.1) | copy-done | bytes 88
  1.3 0.0 copy-start
  1.3 0.7 %copy-done = bf16[2,128,32]{1,2,0:T(8,128)(2,1)S(1)} copy-done((bf16[2,128,32]{1,2,0:T(8,128)(2,1)S(1)}, bf16[2,128,32]{1,2,0:T(8,128)(2,1)}, u32[]{:S(2)}) %copy-start) | copy-done | bytes 16408
  2.0 31.0 %shard_map.58 = (bf16[2,32,128]{2,1,0:T(8,128)(2,1)S(1)}, f32[8,2,128,128]{3,2,1,0:T(8,128)S(1)}, f32[8,2,128,128]{3,2,1,0:T(8,128)S(1)}) custom-call(s32[16]{0:T(128)S(1)} %copy-done.1, bf16[2,32,128]{2,1,0:T(8,128)(2,1)S(1)} %bitcast.2, f32[8,2,128,128]{3,2,1,0:T(8,128)} %prev_hbm.1), custom_call_target="tpu_custom_call" | custom-call | tf_op jit(solution)/shard_map/pallas_call | solution.py:323
  33.0 1.3 %shard_map.59 = (bf16[2,32,128]{2,1,0:T(8,128)(2,1)}, f32[8,2,128,128]{3,2,1,0:T(8,128)}, f32[8,2,128,128]{3,2,1,0:T(8,128)}) custom-call(bf16[2,32,128]{2,1,0:T(8,128)(2,1)S(1)} %get-tuple-element.9.upd, f32[8,2,128,128]{3,2,1,0:T(8,128)S(1)} %get-tuple-element.10.nst, f32[8,2,128,128]{3,2,1,0:T(8,128)S(1)} %get-tuple-element.11.inv), custom_call_target="tpu_custom_call" | custom-call | tf_op jit(solution)/shard_map/pallas_call | solution.py:350
Async XLA Ops:
  0.6 0.7 %copy-start.1 = (s32[16]{0:T(128)S(1)}, s32[16]{0:T(128)}, u32[]{:S(2)}) copy-start(s32[16]{0:T(128)} %owner_ref.1) | copy-start | bytes 196
  1.3 0.7 %copy-start = (bf16[2,128,32]{1,2,0:T(8,128)(2,1)S(1)}, bf16[2,128,32]{1,2,0:T(8,128)(2,1)}, u32[]{:S(2)}) copy-start(bf16[2,128,32]{1,2,0:T(8,128)(2,1)} %param.3) | copy-start | bytes 49156
